TPU v7x, 32 devices: a whole 2x2x4 slice. The times are simulated.
32 devices in a mesh: space: 16 (over z, y, core), tensor: 2 (over x).
Axes of the slice: x: 2, y: 2, z: 4, core: 2. Of those that a mesh axis runs over, the one named last changes fastest.
Arguments:
- tokens: bfloat16 [14336, 1024], P('space', 'tensor'), may hold values from -6 to 6
- first_weight: bfloat16 [1024, 1024], P(None, 'tensor'), may hold values from -0.1875 to 0.1875
- second_weight: bfloat16 [1024, 1024], P(None, 'tensor'), may hold values from -0.1875 to 0.1875
- head_weight: bfloat16 [352, 1024], P('tensor'), may hold values from -0.1875 to 0.1875
- targets: float32 [352, 14336], P('tensor', 'space'), may hold values from -6 to 6
- land_mask: int32 [4, 14336], P(None, 'space'), may hold values from 0 to 1, as said below
- variable_kind: int32 [88], P('tensor'), may hold values from 0 to 2
- loss_scale: float32 [], replicated, may hold values from 630784 to 5046272
Outputs:
- loss: float32 [], replicated
- token_grad: float32 [14336, 1024], P('space', 'tensor')
- first_grad: float32 [1024, 1024], P('space', 'tensor')
- second_grad: float32 [1024, 1024], P('space', 'tensor')
- head_grad: float32 [352, 1024], P('tensor', 'space')
Inputs may be any that keep to these rules, and one draw needn't show every extreme that they name: `land_mask`: every aligned group of 8 entries along the last dimension holds at least one 1 and one 0. `variable_kind`: 0 scores a variable on all cells, 1 on land cells, 2 on ocean cells.
All inputs are finite; a program needn't handle non-finite values.
Results may differ from a plain program's by a relative error of at most 0.0056.
Values may be sent and summed in bfloat16 or wider, within the bound.
A program may use at most 64 MiB of HBM per device.

v0:
```python
import math
import jax
import jax.numpy as jnp
from jax import lax
from jax.sharding import PartitionSpec as P

V = 88
PP = 4
PROW_DEV = 4
LONP = 224


def slope(z):
    cdf = 0.5 * (1.0 + lax.erf(z / math.sqrt(2.0)))
    return cdf + z * jnp.exp(-0.5 * z * z) / math.sqrt(2.0 * math.pi)


def column_folder(weights, piece):
    return lax.dot_general(
        piece, weights, (((1,), (1,)), ((), ())), preferred_element_type=jnp.float32
    )


def row_folder(weights, piece):
    return lax.dot_general(
        piece, weights, (((0,), (0,)), ((), ())), preferred_element_type=jnp.float32
    )


def per_device(
    tokens, first_weight, second_weight, head_weight, targets, land_mask, variable_kind, loss_scale
):
    count = tokens.shape[0]
    width = first_weight.shape[1]
    kinds = head_weight.shape[0] // PP
    rows_first, rows_second = (
        lax.all_to_all(first_weight, "tensor", split_axis=0, concat_axis=1, tiled=True),
        lax.all_to_all(second_weight, "tensor", split_axis=0, concat_axis=1, tiled=True),
    )
    head_cols = lax.all_to_all(head_weight, "tensor", split_axis=1, concat_axis=0, tiled=True)
    position = lax.axis_index("space") * count + jnp.arange(count, dtype=jnp.int32)
    cell = jnp.arange(PP, dtype=jnp.int32)
    lat_row = 2 * (position // LONP)[None, :] + (cell // 2)[:, None]
    nlat = 2 * PROW_DEV * lax.axis_size("space")
    cell_weight = jnp.cos(math.pi / 2.0 * (lat_row.astype(jnp.float32) + 0.5) / nlat)
    land = land_mask.astype(jnp.float32)
    kind = variable_kind[:, None, None]
    valid = jnp.where(kind == 0, 1.0, jnp.where(kind == 1, land[None], 1.0 - land[None]))
    masked = cell_weight[None] * valid
    local_weight = jnp.sum(masked, axis=(1, 2))
    weight_sum = lax.psum(local_weight, "space")
    full_in = lax.all_gather(tokens, "tensor", axis=1, tiled=True)
    pre_one = jnp.dot(full_in, first_weight, preferred_element_type=jnp.float32)
    hidden_one = jax.nn.gelu(pre_one, approximate=False).astype(jnp.bfloat16)
    full_one = lax.all_gather(hidden_one, "tensor", axis=1, tiled=True)
    pre_two = jnp.dot(full_one, second_weight, preferred_element_type=jnp.float32)
    hidden_two = jax.nn.gelu(pre_two, approximate=False).astype(jnp.bfloat16)
    full_two = lax.all_gather(hidden_two, "tensor", axis=1, tiled=True)
    predicted = lax.dot_general(
        head_weight, full_two, (((1,), (1,)), ((), ())), preferred_element_type=jnp.float32
    )
    error = predicted.reshape(kinds, PP, count) - targets.reshape(kinds, PP, count)
    local_error = jnp.sum(masked * error * error, axis=(1, 2))
    error_sum = lax.psum(local_error, "space")
    root = jnp.sqrt(error_sum / weight_sum + 1e-06)
    loss = lax.psum(jnp.sum(root), "tensor") / V
    coef = loss_scale / (V * root * weight_sum)
    grad_pred = (
        (coef[:, None, None] * masked * error).reshape(kinds * PP, count).astype(jnp.bfloat16)
    )
    back_two = row_folder(head_cols, lax.all_gather(grad_pred, "tensor", axis=0, tiled=True))
    head_term = jnp.dot(grad_pred, full_two, preferred_element_type=jnp.float32)
    head_grad = lax.psum_scatter(head_term, "space", scatter_dimension=1, tiled=True)
    grad_two = (back_two * slope(pre_two)).astype(jnp.bfloat16)
    back_one = column_folder(rows_second, lax.all_gather(grad_two, "tensor", axis=1, tiled=True))
    grad_one = (back_one * slope(pre_one)).astype(jnp.bfloat16)
    joined = lax.psum_scatter(
        jnp.concatenate(
            [
                lax.dot_general(
                    full_one, grad_two, (((0,), (0,)), ((), ())), preferred_element_type=jnp.float32
                ),
                lax.dot_general(
                    full_in, grad_one, (((0,), (0,)), ((), ())), preferred_element_type=jnp.float32
                ),
            ],
            axis=1,
        ),
        "space",
        scatter_dimension=0,
        tiled=True,
    )
    second_grad = joined[:, :width]
    first_grad = joined[:, width:]
    token_grad = column_folder(rows_first, lax.all_gather(grad_one, "tensor", axis=1, tiled=True))
    return (loss, token_grad, first_grad, second_grad, head_grad)


def solution(mesh):
    return jax.shard_map(
        per_device,
        mesh=mesh,
        in_specs=(
            P("space", "tensor"),
            P(None, "tensor"),
            P(None, "tensor"),
            P("tensor", None),
            P("tensor", "space"),
            P(None, "space"),
            P("tensor"),
            P(),
        ),
        out_specs=(
            P(),
            P("space", "tensor"),
            P("space", "tensor"),
            P("space", "tensor"),
            P("tensor", "space"),
        ),
        check_vma=False,
    )
```

profile of v0, /device:TPU:0, one launch (start us, length us, event | category | flops | bytes accessed | tf_op | source)
XLA Modules:
  0.0 390.4 jit_solution(11387166332372937541)
XLA Ops:
  7.2 0.7 all-gather.6.cloned.1.call-update
  8.0 34.5 %all-gather.6.cloned.1.call-done = bf16[896,1024]{1,0:T(8,128)(2,1)} async-done(((bf16[896,512]{1,0:T(8,128)(2,1)}), bf16[896,1024]{1,0:T(8,128)(2,1)}) %all-gather.6.cloned.1.call-update) | async-done | bytes 1835024 | tf_op jit(solution)/shard_map/all_gather | solution.py:52
  42.4 8.0 %fusion.2 = (bf16[896,512]{1,0:T(8,128)(2,1)}, f32[896,512]{1,0:T(8,128)}) fusion(bf16[896,1024]{1,0:T(8,128)(2,1)} %all-gather.6.cloned.1.call-done, bf16[1024,512]{1,0:T(8,128)(2,1)} %param.9), kind=kOutput, calls=%fused_computation.7 | convolution fusion | flops 969342976 | bytes 5636096 | tf_op jit(solution)/shard_map/dot_general | solution.py:53
  50.5 30.2 %all-gather.8.cloned.1.call-done = bf16[896,1024]{1,0:T(8,128)(2,1)} async-done(((bf16[896,512]{1,0:T(8,128)(2,1)}), bf16[896,1024]{1,0:T(8,128)(2,1)}) %all-gather.8.cloned.1.call-update) | async-done | bytes 1835024 | tf_op jit(solution)/shard_map/all_gather | solution.py:55
  80.7 7.5 %fusion.5 = (bf16[896,512]{1,0:T(8,128)(2,1)}, f32[896,512]{1,0:T(8,128)}) fusion(bf16[896,1024]{1,0:T(8,128)(2,1)} %all-gather.8.cloned.1.call-done, bf16[1024,512]{1,0:T(8,128)(2,1)S(1)} %copy-done.4), kind=kOutput, calls=%fused_computation.10 | convolution fusion | flops 969342976 | bytes 5636096 | tf_op jit(solution)/shard_map/dot_general | solution.py:56
  88.2 0.8 copy.33
  89.0 4.2 %all-to-all-start = ((bf16[176,2,512]{2,0,1:T(8,128)(2,1)}), bf16[176,2,512]{2,0,1:T(8,128)(2,1)}, u32[]{:S(2)}, u32[]{:S(2)}) async-start(bf16[176,2,512]{2,0,1:T(8,128)(2,1)} %bitcast.37), calls=%async_computation | async-start | bytes 720896 | tf_op jit(solution)/shard_map/all_to_all | solution.py:40
  93.3 0.2 multiply_cosine_fusion
  93.5 0.1 mul.116
  93.6 0.2 mul.117
  93.8 0.1 broadcast_in_dim.68
  93.9 0.2 broadcast_in_dim.69
  94.1 0.1 broadcast_in_dim.70
  94.2 0.2 broadcast_in_dim.71
  94.5 0.1 broadcast_in_dim.65
  94.5 0.1 broadcast_in_dim.66
  94.7 0.1 broadcast_in_dim.61
  94.7 0.1 broadcast_in_dim.62
  95.5 0.8 multiply_reduce_fusion
  96.3 23.1 %all-gather.10.cloned.1.call-done = bf16[896,1024]{1,0:T(8,128)(2,1)} async-done(((bf16[896,512]{1,0:T(8,128)(2,1)}), bf16[896,1024]{1,0:T(8,128)(2,1)}) %all-gather.10.cloned.1.call-update) | async-done | bytes 1835024 | tf_op jit(solution)/shard_map/all_gather | solution.py:58
  119.4 2.6 fusion.33
  122.0 0.1 reduce_sum.35
  122.1 0.1 reduce_sum.36
  122.2 33.2 %all-reduce = (f32[44]{0:T(128)S(1)}, f32[44]{0:T(128)S(1)}) all-reduce(f32[44]{0:T(128)S(1)} %reduce_sum.36, f32[44]{0:T(128)S(1)} %multiply_reduce_fusion), channel_id=1, replica_groups=mesh['space'=16,'tensor'=2] {'space'}, use_global_device_ids=true, to_apply=%region_2.3 | all-reduce | flops 88 | bytes 704 | tf_op jit(solution)/shard_map/psum | solution.py:64
  155.4 0.1 mul.131
  155.5 0.1 mul.132
  155.6 0.2 multiply_convert_fusion
  155.8 7.6 %all_gather.21 = bf16[352,896]{1,0:T(8,128)(2,1)S(1)} all-gather(bf16[176,896]{1,0:T(8,128)(2,1)S(1)} %multiply_convert_fusion), channel_id=1, replica_groups=mesh['space'=16,'tensor'=2] {'tensor'}, dimensions={0}, use_global_device_ids=true | all-gather | bytes 946176 | tf_op jit(solution)/shard_map/all_gather | solution.py:71
  163.4 3.7 fusion.11
  167.2 22.7 %all_to_all.57 = bf16[2,512,512]{2,1,0:T(8,128)(2,1)S(1)} all-to-all(bf16[2,512,512]{2,1,0:T(8,128)(2,1)S(1)} %bitcast.41), channel_id=1, replica_groups=mesh['space'=16,'tensor'=2] {'tensor'}, dimensions={0} | all-to-all | bytes 2097152 | tf_op jit(solution)/shard_map/all_to_all | solution.py:38
  189.9 0.5 copy.23
  190.4 8.6 %all-gather.12.cloned.1.call-done = bf16[896,1024]{1,0:T(8,128)(2,1)} async-done(((bf16[896,512]{1,0:T(8,128)(2,1)}), bf16[896,1024]{1,0:T(8,128)(2,1)}) %all-gather.12.cloned.1.call-update) | async-done | bytes 1835024 | tf_op jit(solution)/shard_map/all_gather | solution.py:75
  199.0 4.6 %fusion.17 = bf16[896,512]{1,0:T(8,128)(2,1)} fusion(f32[896,512]{1,0:T(8,128)} %get-tuple-element.36, bf16[896,1024]{1,0:T(8,128)(2,1)} %all-gather.12.cloned.1.call-done, bf16[512,1024]{0,1:T(8,128)(2,1)S(1)} %bitcast.44), kind=kOutput, calls=%fused_computation.22 | convolution fusion | flops 944111616 | bytes 5636096 | tf_op jit(solution)/shard_map/dot_general | solution.py:19
  203.7 3.2 fusion.38
  206.8 1.3 convolution_bitcast_fusion
  208.1 2.5 pad_maximum_fusion
  210.6 5.5 %copy.27 = f32[1024,1024]{1,0:T(8,128)} copy(f32[1024,1024]{0,1:T(8,128)} %pad_maximum_fusion) | data formatting | bytes 8388608
  216.2 3.7 all-to-all-start.2
  219.9 0.0 reduce-scatter.5.cloned.1.call-start
  220.0 1.9 fusion.39
  221.9 0.6 reduce_sum.38
  222.5 22.4 %all-to-all-done.2 = bf16[2,512,512]{2,1,0:T(8,128)(2,1)S(1)} async-done(((bf16[2,512,512]{2,1,0:T(8,128)(2,1)}), bf16[2,512,512]{2,1,0:T(8,128)(2,1)S(1)}, u32[]{:S(2)}, u32[]{:S(2)}) %all-to-all-start.2) | async-done | bytes 1048608 | tf_op jit(solution)/shard_map/all_to_all | solution.py:37
  244.9 0.5 copy.24
  245.4 5.6 %psum.23 = f32[]{:T(128)} all-reduce(f32[]{:T(128)} %reduce_sum.38), channel_id=1, replica_groups=mesh['space'=16,'tensor'=2] {'tensor'}, use_global_device_ids=true, to_apply=%region_6.7 | all-reduce | flops 1 | bytes 8 | tf_op jit(solution)/shard_map/psum | solution.py:66
  251.7 3.9 fusion.37
  255.5 66.0 %reduce-scatter.7.cloned.1.call-done = f32[64,1024]{1,0:T(8,128)} async-done(((f32[1024,1024]{1,0:T(8,128)}), f32[64,1024]{1,0:T(8,128)}) %reduce-scatter.7.cloned.1.call-update) | async-done | bytes 262160
  321.5 1.7 fusion.36
  323.2 59.2 %reduce-scatter.5.cloned.1.call-done = f32[176,64]{0,1:T(8,128)} async-done(((f32[176,1024]{0,1:T(8,128)}), f32[176,64]{0,1:T(8,128)}) %reduce-scatter.5.cloned.1.call-update) | async-done | bytes 45072 | tf_op jit(solution)/shard_map/reduce_scatter | solution.py:73
  (35 shorter events, 0.5 us)
Async XLA Ops:
  7.2 35.2 %all-gather.6.cloned.1.call-start = ((), (), s32[]{:S(2)}) async-start(), calls=%async_computation.5 | async-start | bytes 2752512 | tf_op jit(solution)/shard_map/all_gather | solution.py:52
  7.9 72.8 %copy-start.4 = (bf16[1024,512]{1,0:T(8,128)(2,1)S(1)}, bf16[1024,512]{1,0:T(8,128)(2,1)}, u32[]{:S(2)}) copy-start(bf16[1024,512]{1,0:T(8,128)(2,1)} %param.10) | copy-start | bytes 3145732
  7.9 72.8 %all-gather.8.cloned.1.call-start = ((), (), s32[]{:S(2)}) async-start(), calls=%async_computation.6 | async-start | bytes 2752512 | tf_op jit(solution)/shard_map/all_gather | solution.py:55
  50.4 37.8 %copy-start.3 = (bf16[176,1024]{1,0:T(8,128)(2,1)S(1)}, bf16[176,1024]{1,0:T(8,128)(2,1)}, u32[]{:S(2)}) copy-start(bf16[176,1024]{1,0:T(8,128)(2,1)} %param.11) | copy-start | bytes 1081348
  50.4 69.0 %all-gather.10.cloned.1.call-start = ((), (), s32[]{:S(2)}) async-start(), calls=%async_computation.7 | async-start | bytes 2752512 | tf_op jit(solution)/shard_map/all_gather | solution.py:58
  88.2 5.0 %copy-start.6 = (s32[4,896]{1,0:T(4,128)S(1)}, s32[4,896]{1,0:T(4,128)}, u32[]{:S(2)}) copy-start(s32[4,896]{1,0:T(4,128)} %param.13) | copy-start | bytes 43012
  89.0 74.4 %all-to-all-start = ((bf16[176,2,512]{2,0,1:T(8,128)(2,1)}), bf16[176,2,512]{2,0,1:T(8,128)(2,1)}, u32[]{:S(2)}, u32[]{:S(2)}) async-start(bf16[176,2,512]{2,0,1:T(8,128)(2,1)} %bitcast.37), calls=%async_computation | async-start | bytes 720896 | tf_op jit(solution)/shard_map/all_to_all | solution.py:40
  93.2 105.8 %all-gather.12.cloned.1.call-start = ((), (), s32[]{:S(2)}) async-start(), calls=%async_computation.8 | async-start | bytes 2752512 | tf_op jit(solution)/shard_map/all_gather | solution.py:75
  93.8 0.7 copy-start.7
  163.4 3.8 copy-start.5
  167.2 84.5 %all-gather.14.cloned.1.call-start = ((), (), s32[]{:S(2)}) async-start(), calls=%async_computation.9 | async-start | bytes 2752512 | tf_op jit(solution)/shard_map/all_gather | solution.py:95
  203.6 3.2 copy-start.1
  203.6 3.2 copy-start.2
  203.6 117.9 %reduce-scatter.7.cloned.1.call-start = ((), (), s32[]{:S(2)}) async-start(), calls=%async_computation.11 | async-start | bytes 4456448
  216.2 3.8 copy-start
  216.2 28.7 %all-to-all-start.2 = ((bf16[2,512,512]{2,1,0:T(8,128)(2,1)}), bf16[2,512,512]{2,1,0:T(8,128)(2,1)S(1)}, u32[]{:S(2)}, u32[]{:S(2)}) async-start(bf16[2,512,512]{2,1,0:T(8,128)(2,1)} %bitcast.42), calls=%async_computation.2 | async-start | bytes 2097152 | tf_op jit(solution)/shard_map/all_to_all | solution.py:37
  219.9 162.5 %reduce-scatter.5.cloned.1.call-start = ((), (), s32[]{:S(2)}) async-start(), calls=%async_computation.10 | async-start | bytes 1114112 | tf_op jit(solution)/shard_map/reduce_scatter | solution.py:73
Sparse Core Ops, SparseCore 0:
  9.5 32.8 all-gather.5
  50.5 30.1 all-gather.7
  88.3 31.0 all-gather.9
  167.3 31.6 all-gather.11
  203.7 40.9 all-gather.13
  248.5 72.9 reduce-scatter.6
  325.7 56.6 reduce-scatter.4
where the time goes:
time: 391 us; the launch traced here: 390 us
  waiting for transfers between devices  245 us (63%)
  blocking collectives  69.1 us (18%)
  matrix products  36.5 us (9%)
  between operations  16.8 us (4%)
  local copies, waits for them, and re-layouts  10.7 us (3%)
  starting transfers between devices  8.16 us (2%)
  other arithmetic  4.37 us (1%)
    unnamed x8, waiting for transfers between devices  66.7 us
    reduce_scatter x1, waiting for transfers between devices, per_device(): lax.psum_scatter(head_term, 'space', scatter_dimension=1, tiled=True)  59.2 us
    all_gather x1, waiting for transfers between devices, per_device(): full_in = lax.all_gather(tokens, 'tensor', axis=1, tiled=True)  34.5 us
    psum x1, blocking collectives, per_device(): error_sum = lax.psum(local_error, 'space')  33.2 us
    all_gather x1, waiting for transfers between devices, per_device(): full_one = lax.all_gather(hidden_one, 'tensor', axis=1, tiled=True)  30.2 us
    all_gather x1, waiting for transfers between devices, per_device(): full_two = lax.all_gather(hidden_two, 'tensor', axis=1, tiled=True)  23.1 us
    all_to_all x1, blocking collectives, per_device(): lax.all_to_all(second_weight, 'tensor', split_axis=0, concat_axis=1, tile...  22.7 us
    all_to_all x1, waiting for transfers between devices, per_device(): lax.all_to_all(first_weight, 'tensor', split_axis=0, concat_axis=1, tiled...  22.4 us
  transfers between devices with their start and end apart: 9, of which 7 were waited for; matrix products, arithmetic and copies ran while one was open for 7% of the time, Pallas kernels for 0%

commit v1 on v0

--- a/solution.py
+++ b/solution.py
@@ -34,7 +34,12 @@
     width = first_weight.shape[1]
     kinds = head_weight.shape[0] // PP
     rows_first, rows_second = (
-        lax.all_to_all(first_weight, "tensor", split_axis=0, concat_axis=1, tiled=True),
+        jnp.concatenate(
+            lax.all_to_all(
+                jnp.stack(jnp.split(first_weight, lax.axis_size("tensor"), axis=0)), "tensor", 0, 0
+            ),
+            axis=1,
+        ),
         lax.all_to_all(second_weight, "tensor", split_axis=0, concat_axis=1, tiled=True),
     )
     head_cols = lax.all_to_all(head_weight, "tensor", split_axis=1, concat_axis=0, tiled=True)

time: 391 us -> 390 us (level)
  waiting for transfers between devices: 245 us -> 227 us
  blocking collectives: 69.1 us -> 83.8 us
    all_to_all x1, waiting for transfers between devices: 22.4 us -> 0.01 us  [per_device(): lax.all_to_all(jnp.stack(jnp.split(first_weight, lax.axis_size('tensor'),...]
    psum x1, blocking collectives: 5.57 us -> 20.4 us  [per_device(): loss = lax.psum(jnp.sum(root), 'tensor') / V]
    unnamed x8, waiting for transfers between devices: 66.7 us -> 71.6 us
  transfers between devices with their start and end apart: 9 -> 9, of which waited for: 7 -> 6; matrix products, arithmetic and copies ran while one was open for 7% -> 7% of each run, Pallas kernels for 0% -> 0%
where the time goes in v1:
time: 390 us
  waiting for transfers between devices  227 us (58%)
  blocking collectives  83.8 us (21%)
  matrix products  36.5 us (9%)
  between operations  16.8 us (4%)
  local copies, waits for them, and re-layouts  11.9 us (3%)
  starting transfers between devices  8.01 us (2%)
  other arithmetic  5.44 us (1%)
    unnamed x8, waiting for transfers between devices  71.6 us
    reduce_scatter x1, waiting for transfers between devices, per_device(): lax.psum_scatter(head_term, 'space', scatter_dimension=1, tiled=True)  59.1 us
    all_gather x1, waiting for transfers between devices, per_device(): full_in = lax.all_gather(tokens, 'tensor', axis=1, tiled=True)  34.5 us
    psum x1, blocking collectives, per_device(): error_sum = lax.psum(local_error, 'space')  33.2 us
    all_gather x1, waiting for transfers between devices, per_device(): full_one = lax.all_gather(hidden_one, 'tensor', axis=1, tiled=True)  30.2 us
    all_gather x1, waiting for transfers between devices, per_device(): full_two = lax.all_gather(hidden_two, 'tensor', axis=1, tiled=True)  23.1 us
    all_to_all x1, blocking collectives, per_device(): lax.all_to_all(second_weight, 'tensor', split_axis=0, concat_axis=1, tile...  22.7 us
    psum x1, blocking collectives, per_device(): loss = lax.psum(jnp.sum(root), 'tensor') / V  20.4 us
  transfers between devices with their start and end apart: 9, of which 6 were waited for; matrix products, arithmetic and copies ran while one was open for 7% of the time, Pallas kernels for 0%

profile of v1, /device:TPU:0, one launch (start us, length us, event | category | flops | bytes accessed | tf_op | source)
XLA Modules:
  0.0 389.6 jit_solution(16165921942225958069)
XLA Ops:
  7.2 0.7 all-gather.6.cloned.1.call-update
  8.0 34.5 %all-gather.6.cloned.1.call-done = bf16[896,1024]{1,0:T(8,128)(2,1)} async-done(((bf16[896,512]{1,0:T(8,128)(2,1)}), bf16[896,1024]{1,0:T(8,128)(2,1)}) %all-gather.6.cloned.1.call-update) | async-done | bytes 1835024 | tf_op jit(solution)/shard_map/all_gather | solution.py:57
  42.4 8.0 %fusion.2 = (bf16[896,512]{1,0:T(8,128)(2,1)}, f32[896,512]{1,0:T(8,128)}) fusion(bf16[896,1024]{1,0:T(8,128)(2,1)} %all-gather.6.cloned.1.call-done, bf16[1024,512]{1,0:T(8,128)(2,1)} %param.9), kind=kOutput, calls=%fused_computation.7 | convolution fusion | flops 969342976 | bytes 5636096 | tf_op jit(solution)/shard_map/dot_general | solution.py:58
  50.5 30.2 %all-gather.8.cloned.1.call-done = bf16[896,1024]{1,0:T(8,128)(2,1)} async-done(((bf16[896,512]{1,0:T(8,128)(2,1)}), bf16[896,1024]{1,0:T(8,128)(2,1)}) %all-gather.8.cloned.1.call-update) | async-done | bytes 1835024 | tf_op jit(solution)/shard_map/all_gather | solution.py:60
  80.7 7.5 %fusion.5 = (bf16[896,512]{1,0:T(8,128)(2,1)}, f32[896,512]{1,0:T(8,128)}) fusion(bf16[896,1024]{1,0:T(8,128)(2,1)} %all-gather.8.cloned.1.call-done, bf16[1024,512]{1,0:T(8,128)(2,1)S(1)} %copy-done.4), kind=kOutput, calls=%fused_computation.10 | convolution fusion | flops 969342976 | bytes 5636096 | tf_op jit(solution)/shard_map/dot_general | solution.py:61
  88.2 0.8 copy.39
  89.0 4.1 %all-to-all-start = ((bf16[176,2,512]{2,0,1:T(8,128)(2,1)}), bf16[176,2,512]{2,0,1:T(8,128)(2,1)}, u32[]{:S(2)}, u32[]{:S(2)}) async-start(bf16[176,2,512]{2,0,1:T(8,128)(2,1)} %bitcast.39), calls=%async_computation | async-start | bytes 720896 | tf_op jit(solution)/shard_map/all_to_all | solution.py:45
  93.3 0.2 multiply_cosine_fusion
  93.4 0.1 mul.116
  93.5 0.2 mul.117
  93.8 0.1 broadcast_in_dim.68
  93.9 0.2 broadcast_in_dim.69
  94.1 0.1 broadcast_in_dim.70
  94.2 0.2 broadcast_in_dim.71
  94.4 0.1 broadcast_in_dim.65
  94.5 0.1 broadcast_in_dim.66
  94.6 0.1 broadcast_in_dim.61
  94.7 0.1 broadcast_in_dim.62
  95.5 0.8 multiply_reduce_fusion
  96.2 23.1 %all-gather.10.cloned.1.call-done = bf16[896,1024]{1,0:T(8,128)(2,1)} async-done(((bf16[896,512]{1,0:T(8,128)(2,1)}), bf16[896,1024]{1,0:T(8,128)(2,1)}) %all-gather.10.cloned.1.call-update) | async-done | bytes 1835024 | tf_op jit(solution)/shard_map/all_gather | solution.py:63
  119.4 2.6 fusion.33
  121.9 0.1 reduce_sum.35
  122.0 0.1 reduce_sum.36
  122.2 33.2 %all-reduce = (f32[44]{0:T(128)S(1)}, f32[44]{0:T(128)S(1)}) all-reduce(f32[44]{0:T(128)S(1)} %reduce_sum.36, f32[44]{0:T(128)S(1)} %multiply_reduce_fusion), channel_id=1, replica_groups=mesh['space'=16,'tensor'=2] {'space'}, use_global_device_ids=true, to_apply=%region_2.3 | all-reduce | flops 88 | bytes 704 | tf_op jit(solution)/shard_map/psum | solution.py:69
  155.5 0.1 mul.132
  155.6 0.2 multiply_convert_fusion
  155.7 7.6 %all_gather.21 = bf16[352,896]{1,0:T(8,128)(2,1)S(1)} all-gather(bf16[176,896]{1,0:T(8,128)(2,1)S(1)} %multiply_convert_fusion), channel_id=1, replica_groups=mesh['space'=16,'tensor'=2] {'tensor'}, dimensions={0}, use_global_device_ids=true | all-gather | bytes 946176 | tf_op jit(solution)/shard_map/all_gather | solution.py:76
  163.4 3.7 fusion.11
  167.2 22.7 %all_to_all.43 = bf16[2,512,512]{2,1,0:T(8,128)(2,1)S(1)} all-to-all(bf16[2,512,512]{2,1,0:T(8,128)(2,1)S(1)} %bitcast.44), channel_id=1, replica_groups=mesh['space'=16,'tensor'=2] {'tensor'}, dimensions={0} | all-to-all | bytes 2097152 | tf_op jit(solution)/shard_map/all_to_all | solution.py:43
  189.8 0.5 copy.26
  190.4 8.6 %all-gather.12.cloned.1.call-done = bf16[896,1024]{1,0:T(8,128)(2,1)} async-done(((bf16[896,512]{1,0:T(8,128)(2,1)}), bf16[896,1024]{1,0:T(8,128)(2,1)}) %all-gather.12.cloned.1.call-update) | async-done | bytes 1835024 | tf_op jit(solution)/shard_map/all_gather | solution.py:80
  198.9 4.6 %fusion.17 = bf16[896,512]{1,0:T(8,128)(2,1)} fusion(f32[896,512]{1,0:T(8,128)} %get-tuple-element.38, bf16[896,1024]{1,0:T(8,128)(2,1)} %all-gather.12.cloned.1.call-done, bf16[512,1024]{0,1:T(8,128)(2,1)S(1)} %bitcast.46), kind=kOutput, calls=%fused_computation.22 | convolution fusion | flops 944111616 | bytes 5636096 | tf_op jit(solution)/shard_map/dot_general | solution.py:19
  203.6 3.2 fusion.39
  206.8 1.3 convolution_bitcast_fusion
  208.1 2.5 pad_maximum_fusion
  210.6 5.5 %copy.31 = f32[1024,1024]{1,0:T(8,128)} copy(f32[1024,1024]{0,1:T(8,128)} %pad_maximum_fusion) | data formatting | bytes 8388608
  216.2 1.2 copy-done.6
  217.4 0.2 copy.34
  217.6 0.2 copy.33
  217.9 1.1 pad_maximum_fusion.1
  218.9 3.6 all-to-all-start.2
  222.6 1.9 fusion.40
  224.5 0.6 reduce_sum.38
  225.1 20.4 %psum.23 = f32[]{:T(128)} all-reduce(f32[]{:T(128)} %reduce_sum.38), channel_id=1, replica_groups=mesh['space'=16,'tensor'=2] {'tensor'}, use_global_device_ids=true, to_apply=%region_6.7 | all-reduce | flops 1 | bytes 8 | tf_op jit(solution)/shard_map/psum | solution.py:71
  246.1 3.9 fusion.38
  250.0 70.8 %reduce-scatter.7.cloned.1.call-done = f32[64,1024]{1,0:T(8,128)} async-done(((f32[1024,1024]{1,0:T(8,128)}), f32[64,1024]{1,0:T(8,128)}) %reduce-scatter.7.cloned.1.call-update) | async-done | bytes 262160
  320.8 1.7 fusion.37
  322.5 59.1 %reduce-scatter.5.cloned.1.call-done = f32[176,64]{0,1:T(8,128)} async-done(((f32[176,1024]{0,1:T(8,128)}), f32[176,64]{0,1:T(8,128)}) %reduce-scatter.5.cloned.1.call-update) | async-done | bytes 45072 | tf_op jit(solution)/shard_map/reduce_scatter | solution.py:78
  (40 shorter events, 0.7 us)
Async XLA Ops:
  7.2 35.2 %all-gather.6.cloned.1.call-start = ((), (), s32[]{:S(2)}) async-start(), calls=%async_computation.5 | async-start | bytes 2752512 | tf_op jit(solution)/shard_map/all_gather | solution.py:57
  7.9 72.8 %copy-start.4 = (bf16[1024,512]{1,0:T(8,128)(2,1)S(1)}, bf16[1024,512]{1,0:T(8,128)(2,1)}, u32[]{:S(2)}) copy-start(bf16[1024,512]{1,0:T(8,128)(2,1)} %param.10) | copy-start | bytes 3145732
  7.9 72.8 %all-gather.8.cloned.1.call-start = ((), (), s32[]{:S(2)}) async-start(), calls=%async_computation.6 | async-start | bytes 2752512 | tf_op jit(solution)/shard_map/all_gather | solution.py:60
  50.4 37.8 %copy-start.3 = (bf16[176,1024]{1,0:T(8,128)(2,1)S(1)}, bf16[176,1024]{1,0:T(8,128)(2,1)}, u32[]{:S(2)}) copy-start(bf16[176,1024]{1,0:T(8,128)(2,1)} %param.11) | copy-start | bytes 1081348
  50.4 68.9 %all-gather.10.cloned.1.call-start = ((), (), s32[]{:S(2)}) async-start(), calls=%async_computation.7 | async-start | bytes 2752512 | tf_op jit(solution)/shard_map/all_gather | solution.py:63
  88.2 5.0 %copy-start.7 = (s32[4,896]{1,0:T(4,128)S(1)}, s32[4,896]{1,0:T(4,128)}, u32[]{:S(2)}) copy-start(s32[4,896]{1,0:T(4,128)} %param.13) | copy-start | bytes 43012
  89.0 74.4 %all-to-all-start = ((bf16[176,2,512]{2,0,1:T(8,128)(2,1)}), bf16[176,2,512]{2,0,1:T(8,128)(2,1)}, u32[]{:S(2)}, u32[]{:S(2)}) async-start(bf16[176,2,512]{2,0,1:T(8,128)(2,1)} %bitcast.39), calls=%async_computation | async-start | bytes 720896 | tf_op jit(solution)/shard_map/all_to_all | solution.py:45
  93.1 105.8 %all-gather.12.cloned.1.call-start = ((), (), s32[]{:S(2)}) async-start(), calls=%async_computation.8 | async-start | bytes 2752512 | tf_op jit(solution)/shard_map/all_gather | solution.py:80
  93.8 0.7 copy-start.8
  163.4 3.8 copy-start.5
  167.1 79.0 %all-gather.14.cloned.1.call-start = ((), (), s32[]{:S(2)}) async-start(), calls=%async_computation.9 | async-start | bytes 2752512 | tf_op jit(solution)/shard_map/all_gather | solution.py:100
  203.6 3.2 copy-start.1
  203.6 3.2 copy-start.2
  203.6 117.2 %reduce-scatter.7.cloned.1.call-start = ((), (), s32[]{:S(2)}) async-start(), calls=%async_computation.11 | async-start | bytes 4456448
  216.1 1.2 copy-start.6
  217.9 4.7 %copy-start = (bf16[896,1024]{1,0:T(8,128)(2,1)S(1)}, bf16[896,1024]{1,0:T(8,128)(2,1)}, u32[]{:S(2)}) copy-start(bf16[896,1024]{1,0:T(8,128)(2,1)} %all-gather.10.cloned.1.call-done) | copy-start | bytes 5505028
  218.9 27.1 %all-to-all-start.2 = ((bf16[2,512,512]{1,2,0:T(8,128)(2,1)}), bf16[2,512,512]{1,2,0:T(8,128)(2,1)S(1)}, u32[]{:S(2)}, u32[]{:S(2)}) async-start(bf16[2,512,512]{1,2,0:T(8,128)(2,1)} %pad_maximum_fusion.1), calls=%async_computation.2 | async-start | bytes 2097152 | tf_op jit(solution)/shard_map/all_to_all | solution.py:38
  222.5 159.1 %reduce-scatter.5.cloned.1.call-start = ((), (), s32[]{:S(2)}) async-start(), calls=%async_computation.10 | async-start | bytes 1114112 | tf_op jit(solution)/shard_map/reduce_scatter | solution.py:78
Sparse Core Ops, SparseCore 0:
  9.5 32.8 all-gather.5
  50.5 30.1 all-gather.7
  88.3 30.9 all-gather.9
  167.2 31.6 all-gather.11
  203.7 38.3 all-gather.13
  245.8 74.9 reduce-scatter.6
  325.0 56.5 reduce-scatter.4
